TPU v7x, 32 devices: a whole 2x2x4 slice. The times are simulated.
32 devices in a mesh: seq: 8 (over z, x), batch: 4 (over y, core).
Axes of the slice: x: 2, y: 2, z: 4, core: 2. Of those that a mesh axis runs over, the one named last changes fastest.
Arguments:
- tokens: bfloat16 [4, 2048, 256], P('batch', 'seq'), may hold values from -6 to 6
- out_grad: bfloat16 [4, 2048, 256], P('batch', 'seq'), may hold values from -6 to 6
- in_weight: bfloat16 [256, 768], replicated, may hold values from -0.375 to 0.375
- out_weight: bfloat16 [256, 256], replicated, may hold values from -0.375 to 0.375
- skip_bias: float32 [256], replicated, may hold values from -4 to 4
- embed_weight: float32 [5, 64], replicated, may hold values from -4 to 4
- embed_bias: float32 [64], replicated, may hold values from -4 to 4
- hidden_weight: float32 [64, 64], replicated, may hold values from -0.75 to 0.75
- hidden_bias: float32 [64], replicated, may hold values from -4 to 4
- filter_weight: float32 [64, 256], replicated, may hold values from -0.75 to 0.75
- sine_freq: float32 [2, 64], replicated, may hold values from 0.5 to 3
- decay_rate: float32 [256], replicated, may hold values from 0.0014990234 to 0.0074951174
Outputs:
- grad_tokens: bfloat16 [4, 2048, 256], P('batch', 'seq')
- grad_in_weight: float32 [256, 768], replicated
- grad_out_weight: float32 [256, 256], replicated
- grad_skip_bias: float32 [256], replicated
- grad_embed_weight: float32 [5, 64], replicated
- grad_embed_bias: float32 [64], replicated
- grad_hidden_weight: float32 [64, 64], replicated
- grad_hidden_bias: float32 [64], replicated
- grad_filter_weight: float32 [64, 256], replicated
- grad_sine_freq: float32 [2, 64], replicated
All inputs are finite; a program needn't handle non-finite values.
Results may differ from a plain program's by a relative error of at most 0.013.
Values may be sent and summed in bfloat16 or wider, within the bound.
A program may use at most 64 MiB of HBM per device.

v0:
```python
import math

import jax
import jax.numpy as jnp
from jax import lax
from jax.sharding import PartitionSpec as P

highest = lax.Precision.HIGHEST


def angle_table(row_count, col_count, period):
    index_product = (
        jnp.arange(row_count, dtype=jnp.int32)[:, None]
        * jnp.arange(col_count, dtype=jnp.int32)[None, :]
        % period
    )
    angles = index_product.astype(jnp.float32) * (2.0 * math.pi / period)
    return (jnp.cos(angles), jnp.sin(angles))


def make_tables(length):
    total = 2 * length
    first_len = 2
    while first_len * first_len < total and total % (2 * first_len) == 0:
        first_len = first_len * 2
    second_len = total // first_len
    outer_cos, outer_sin = angle_table(first_len, first_len, first_len)
    inner_cos, inner_sin = angle_table(second_len, second_len, second_len)
    twist_cos, twist_sin = angle_table(first_len, second_len, total)
    return (outer_cos, outer_sin, inner_cos, inner_sin, twist_cos, twist_sin)


def right_multiply(stack_part, table):
    return jnp.einsum("...km,mj->...kj", stack_part, table, precision=highest)


def spectrum(signal, tables):
    outer_cos, outer_sin, inner_cos, inner_sin, twist_cos, twist_sin = tables
    half_len = outer_cos.shape[0] // 2
    second_len = inner_cos.shape[0]
    blocks = signal.reshape(signal.shape[:-1] + (half_len, second_len))
    real_section = jnp.einsum("kn,...nm->...km", outer_cos[:, :half_len], blocks, precision=highest)
    imag_section = -jnp.einsum(
        "kn,...nm->...km", outer_sin[:, :half_len], blocks, precision=highest
    )
    real_twist = real_section * twist_cos + imag_section * twist_sin
    imag_twist = imag_section * twist_cos - real_section * twist_sin
    real_out = right_multiply(real_twist, inner_cos) + right_multiply(imag_twist, inner_sin)
    imag_out = right_multiply(imag_twist, inner_cos) - right_multiply(real_twist, inner_sin)
    return (real_out, imag_out)


def inverse(spectra, tables):
    real_in, imag_in = spectra
    outer_cos, outer_sin, inner_cos, inner_sin, twist_cos, twist_sin = tables
    first_len = outer_cos.shape[0]
    half_len = first_len // 2
    second_len = inner_cos.shape[0]
    real_section = right_multiply(real_in, inner_cos) - right_multiply(imag_in, inner_sin)
    imag_section = right_multiply(imag_in, inner_cos) + right_multiply(real_in, inner_sin)
    real_twist = real_section * twist_cos - imag_section * twist_sin
    imag_twist = real_section * twist_sin + imag_section * twist_cos
    signal = jnp.einsum("nk,...km->...nm", outer_cos[:half_len], real_twist, precision=highest)
    signal = signal - jnp.einsum(
        "nk,...km->...nm", outer_sin[:half_len], imag_twist, precision=highest
    )
    signal = signal / float(first_len * second_len)
    return signal.reshape(signal.shape[:-2] + (half_len * second_len,))


def multiply(left_pair, right_pair, conjugate):
    left_real, left_imag = left_pair
    right_real, right_imag = right_pair
    if conjugate:
        return (
            left_real * right_real + left_imag * right_imag,
            left_imag * right_real - left_real * right_imag,
        )
    return (
        left_real * right_real - left_imag * right_imag,
        left_real * right_imag + left_imag * right_real,
    )


def embedding(positions, length, band_count):
    scaled = positions / length
    rows_list = [scaled]
    for band_index in range(1, band_count + 1):
        angle = 2.0 * math.pi * band_index * scaled
        rows_list.append(jnp.cos(angle))
        rows_list.append(jnp.sin(angle))
    return jnp.stack(rows_list, axis=0)


def modulation(decay_part, positions, length):
    return 4.0 * jnp.exp(-decay_part[:, None] * positions[None, :]) / math.sqrt(length)


def contract_first(left_side, right_side):
    return lax.dot_general(left_side, right_side, (((0,), (0,)), ((), ())), precision=highest)


def contract_last(left_side, right_side):
    return lax.dot_general(left_side, right_side, (((1,), (1,)), ((), ())), precision=highest)


def mlp_forward(embed_rows, embed_weight, embed_bias, hidden_weight, hidden_bias, sine_freq):
    pre_one = contract_first(embed_weight, embed_rows) + embed_bias[:, None]
    act_one = jnp.sin(sine_freq[0][:, None] * pre_one)
    pre_two = contract_first(hidden_weight, act_one) + hidden_bias[:, None]
    act_two = jnp.sin(sine_freq[1][:, None] * pre_two)
    return (pre_one, act_one, pre_two, act_two)


def filter_values(activations, weight_part, modul):
    return contract_first(weight_part, activations[3]) * modul


def mlp_backward(
    embed_rows, activations, hidden_weight, sine_freq, weight_part, modul, grad_filter
):
    pre_one, act_one, pre_two, act_two = activations
    grad_kernel = grad_filter * modul
    grad_weight_part = contract_last(act_two, grad_kernel)
    grad_act_two = jnp.dot(weight_part, grad_kernel, precision=highest)
    cos_two = jnp.cos(sine_freq[1][:, None] * pre_two)
    grad_pre_two = grad_act_two * sine_freq[1][:, None] * cos_two
    grad_freq_two = jnp.sum(grad_act_two * pre_two * cos_two, axis=1)
    grad_hidden_bias = jnp.sum(grad_pre_two, axis=1)
    grad_hidden_weight = contract_last(act_one, grad_pre_two)
    grad_act_one = jnp.dot(hidden_weight, grad_pre_two, precision=highest)
    cos_one = jnp.cos(sine_freq[0][:, None] * pre_one)
    grad_pre_one = grad_act_one * sine_freq[0][:, None] * cos_one
    grad_freq_one = jnp.sum(grad_act_one * pre_one * cos_one, axis=1)
    grad_embed_bias = jnp.sum(grad_pre_one, axis=1)
    grad_embed_weight = contract_last(embed_rows, grad_pre_one)
    return (
        grad_embed_weight,
        grad_embed_bias,
        grad_hidden_weight,
        grad_hidden_bias,
        grad_weight_part,
        jnp.stack([grad_freq_one, grad_freq_two], axis=0),
    )


def shards(
    tokens,
    out_grad,
    in_weight,
    out_weight,
    skip_bias,
    embed_weight,
    embed_bias,
    hidden_weight,
    hidden_bias,
    filter_weight,
    sine_freq,
    decay_rate,
):
    tokens_local = tokens[0]
    grad_local = out_grad[0]
    pos_dev = tokens_local.shape[0]
    model_width = tokens_local.shape[1]
    seq_count = lax.axis_size("seq")
    batch_count = lax.axis_size("batch")
    length = pos_dev * seq_count
    seq_index = lax.axis_index("seq")
    projected = jnp.dot(tokens_local, in_weight, preferred_element_type=jnp.float32)
    gate_out = projected[:, :model_width].astype(jnp.bfloat16)
    gate_in = projected[:, model_width : 2 * model_width].astype(jnp.bfloat16)
    values_in = projected[:, 2 * model_width :].astype(jnp.bfloat16)
    mixed = (values_in.astype(jnp.float32) * gate_in.astype(jnp.float32)).astype(jnp.bfloat16)
    grad_gated = lax.dot_general(
        grad_local, out_weight, (((1,), (1,)), ((), ())), preferred_element_type=jnp.float32
    ).astype(jnp.bfloat16)
    grad_conv = (grad_gated.astype(jnp.float32) * gate_out.astype(jnp.float32)).astype(jnp.bfloat16)
    bias_part = jnp.sum(grad_conv.astype(jnp.float32) * mixed.astype(jnp.float32), axis=0)
    mixed_rows, grad_rows = (
        lax.all_to_all(mixed.T, "seq", split_axis=0, concat_axis=1, tiled=True),
        lax.all_to_all(grad_conv.T, "seq", split_axis=0, concat_axis=1, tiled=True),
    )
    mixed_chan = mixed_rows[None]
    grad_chan = grad_rows[None]
    chan_dev = model_width // seq_count
    chan_start = seq_index * chan_dev
    all_positions = jnp.arange(length, dtype=jnp.float32)
    band_count = (embed_weight.shape[0] - 1) // 2
    embed_all = embedding(all_positions, length, band_count)
    weight_part = lax.dynamic_slice_in_dim(filter_weight, chan_start, chan_dev, 1)
    decay_part = lax.dynamic_slice_in_dim(decay_rate, chan_start, chan_dev, 0)
    bias_chan = lax.dynamic_slice_in_dim(skip_bias, chan_start, chan_dev, 0)[:, None]
    modul_all = modulation(decay_part, all_positions, length)
    activations = mlp_forward(
        embed_all, embed_weight, embed_bias, hidden_weight, hidden_bias, sine_freq
    )
    filter_chan = filter_values(activations, weight_part, modul_all)
    tables = make_tables(length)
    mixed_float = mixed_chan.astype(jnp.float32)
    grad_float = grad_chan.astype(jnp.float32)
    mixed_spec = spectrum(mixed_float, tables)
    grad_spec = spectrum(grad_float, tables)
    filter_spec = spectrum(filter_chan, tables)
    conv_chan = (
        inverse(multiply(mixed_spec, filter_spec, False), tables) + bias_chan * mixed_float
    ).astype(jnp.bfloat16)
    grad_mixed_chan = (
        inverse(multiply(grad_spec, filter_spec, True), tables) + bias_chan * grad_float
    ).astype(jnp.bfloat16)
    grad_filter_seq = inverse(multiply(grad_spec, mixed_spec, True), tables)
    grad_filter_local = jnp.sum(grad_filter_seq, axis=0)
    conv_rows, grad_mixed_rows = (
        lax.all_to_all(conv_chan[0], "seq", split_axis=1, concat_axis=0, tiled=True),
        lax.all_to_all(grad_mixed_chan[0], "seq", split_axis=1, concat_axis=0, tiled=True),
    )
    conv_float = conv_rows.T.astype(jnp.float32)
    grad_mixed_float = grad_mixed_rows.T.astype(jnp.float32)
    gated = (gate_out.astype(jnp.float32) * conv_float).astype(jnp.bfloat16)
    grad_out_weight = lax.dot_general(
        gated, grad_local, (((0,), (0,)), ((), ())), preferred_element_type=jnp.float32
    )
    grad_gate_out = (grad_gated.astype(jnp.float32) * conv_float).astype(jnp.bfloat16)
    grad_gate_in = (grad_mixed_float * values_in.astype(jnp.float32)).astype(jnp.bfloat16)
    grad_values = (grad_mixed_float * gate_in.astype(jnp.float32)).astype(jnp.bfloat16)
    grad_proj = jnp.concatenate([grad_gate_out, grad_gate_in, grad_values], axis=1)
    grad_tokens = lax.dot_general(
        grad_proj, in_weight, (((1,), (1,)), ((), ())), preferred_element_type=jnp.float32
    ).astype(jnp.bfloat16)
    grad_in_weight = lax.dot_general(
        tokens_local, grad_proj, (((0,), (0,)), ((), ())), preferred_element_type=jnp.float32
    )
    filter_grads = mlp_backward(
        embed_all, activations, hidden_weight, sine_freq, weight_part, modul_all, grad_filter_local
    )
    zero_grad = jnp.zeros((hidden_weight.shape[0], model_width), jnp.float32)
    grad_filter_weight = lax.dynamic_update_slice_in_dim(zero_grad, filter_grads[4], chan_start, 1)
    totals = lax.psum(
        (
            grad_in_weight,
            grad_out_weight,
            bias_part,
            filter_grads[0],
            filter_grads[1],
            filter_grads[2],
            filter_grads[3],
            grad_filter_weight,
            filter_grads[5],
        ),
        ("seq", "batch"),
    )
    grad_scale = 1.0 / math.sqrt(batch_count * length)
    filter_scale = grad_scale / 4.0
    return (
        grad_tokens[None],
        totals[0] * grad_scale,
        totals[1] * grad_scale,
        totals[2] * grad_scale,
        totals[3] * filter_scale,
        totals[4] * filter_scale,
        totals[5] * filter_scale,
        totals[6] * filter_scale,
        totals[7] * filter_scale,
        totals[8] * filter_scale,
    )


def solution(mesh):
    placed = (
        P("batch", "seq", None),
        P("batch", "seq", None),
        P(),
        P(),
        P(),
        P(),
        P(),
        P(),
        P(),
        P(),
        P(),
        P(),
    )
    return jax.shard_map(
        shards,
        mesh=mesh,
        in_specs=placed,
        out_specs=(P("batch", "seq", None), P(), P(), P(), P(), P(), P(), P(), P(), P()),
        check_vma=False,
    )
```

profile of v0, /device:TPU:1, one launch (start us, length us, event | category | flops | bytes accessed | tf_op | source)
XLA Modules:
  0.0 366.4 jit_solution(12775021197319997031)
XLA Ops:
  7.2 1.0 copy-done
  8.2 1.2 convolution_convert_fusion
  9.4 1.0 multiply_reduce_fusion.2
  10.5 6.3 %all-to-all-start = ((bf16[8,32,256]{2,1,0:T(8,128)(2,1)}), bf16[8,32,256]{2,1,0:T(8,128)(2,1)S(1)}, u32[]{:S(2)}, u32[]{:S(2)}) async-start(bf16[8,32,256]{2,1,0:T(8,128)(2,1)} %bitcast.3), calls=%async_computation | async-start | bytes 262144 | tf_op jit(solution)/shard_map/all_to_all | solution.py:180
  21.1 2.4 fusion
  23.5 0.8 copy-done.3
  24.3 2.1 convolution_multiply_fusion
  26.6 1.8 convolution_bitcast_fusion
  28.5 1.8 fusion.1
  30.3 1.9 fusion.59
  32.2 14.1 %fusion.60 = f32[32,64,64]{2,1,0:T(8,128)S(1)} fusion(f32[32,64,64]{1,2,0:T(8,128)S(1)} %convolution_bitcast_fusion, f32[32,64,64]{1,2,0:T(8,128)S(1)} %fusion.1, f32[64,64]{0,1:T(8,128)S(1)} %get-tuple-element.56, f32[64,64]{0,1:T(8,128)S(1)} %get-tuple-element.57), kind=kOutput, calls=%fused_computation.115 | convolution fusion | flops 101113856 | bytes 1605632 | tf_op jit(solution)/shard_map/...km,mj->...kj/dot_general | solution.py:34
  46.3 2.9 convolution_add_fusion.6
  49.8 2.9 convolution_subtract_fusion.4
  52.7 5.4 %all-to-all-start.2 = ((bf16[8,32,256]{2,1,0:T(8,128)(2,1)}), bf16[8,32,256]{2,1,0:T(8,128)(2,1)}, u32[]{:S(2)}, u32[]{:S(2)}) async-start(bf16[8,32,256]{2,1,0:T(8,128)(2,1)} %bitcast.40), calls=%async_computation.2 | async-start | bytes 262144 | tf_op jit(solution)/shard_map/all_to_all | solution.py:181
  58.4 0.7 convolution_bitcast_fusion.2
  59.8 4.7 %all-to-all-done.2 = bf16[8,32,256]{2,1,0:T(8,128)(2,1)} async-done(((bf16[8,32,256]{2,1,0:T(8,128)(2,1)}), bf16[8,32,256]{2,1,0:T(8,128)(2,1)}, u32[]{:S(2)}, u32[]{:S(2)}) %all-to-all-start.2) | async-done | bytes 131104 | tf_op jit(solution)/shard_map/all_to_all | solution.py:181
  64.4 1.6 copy.53
  66.1 1.1 reshape.365
  68.5 1.9 fusion.22
  70.4 1.9 fusion.18
  72.3 1.9 fusion.16
  74.2 1.9 fusion.12
  76.1 2.3 convolution_add_fusion.7
  78.4 1.9 convolution_add_fusion.4
  80.3 1.9 convolution_subtract_fusion.5
  82.2 3.7 multiply_add_fusion
  85.9 3.2 fusion.104
  89.0 3.2 fusion.102
  92.2 3.2 convolution_subtract_fusion
  95.4 3.3 convolution_add_fusion.2
  98.7 3.0 fusion.27
  101.7 3.8 %fusion.5 = f32[1,32,32,64]{3,2,1,0:T(8,128)} fusion(f32[32,64,32]{1,2,0:T(8,128)S(1)} %fusion.27, f32[32,64,64]{1,2,0:T(8,128)S(1)} %convolution_add_fusion.2, f32[32,64,64]{1,2,0:T(8,128)S(1)} %convolution_subtract_fusion, f32[64,64]{0,1:T(8,128)S(1)} %get-tuple-element.56, f32[64,64]{0,1:T(8,128)S(1)} %get-tuple-element.57, f32[64,64]{0,1:T(8,128)S(1)} %fusion.131), kind=kOutput, calls=%fused_computation.29 | convolution fusion | flops 50855936 | bytes 1622016 | tf_op jit(solution)/shard_map/nk,...km->...nm/dot_general | solution.py:64
  105.5 1.2 reduce_sum.52
  106.7 4.1 %fusion.265 = (f32[64]{0:T(128)}, f32[64,2048]{1,0:T(8,128)S(1)}, f32[64]{0:T(128)}) fusion(f32[64,2048]{1,0:T(8,128)} %copy-done.3, f32[64]{0:T(128)S(1)} %get-tuple-element.50, f32[32,2048]{1,0:T(8,128)S(1)} %reduce_sum.52, f32[32]{0:T(128)S(1)} %dynamic-slice_negate_fusion, f32[64,256]{1,0:T(8,128)} %param.21, s32[]{:T(128)S(6)} %select_n.151), kind=kOutput, calls=%fused_computation.324 | convolution fusion | flops 51445632 | bytes 1344388 | tf_op jit(solution)/shard_map/dot_general | solution.py:125
  110.8 2.9 multiply_reduce_fusion.1
  113.7 2.9 fusion.57
  116.6 3.0 fusion.58
  119.6 2.2 fusion.158
  121.8 3.2 fusion.108
  125.0 3.6 fusion.106
  128.6 3.2 convolution_subtract_fusion.1
  131.8 3.2 convolution_add_fusion.3
  134.9 3.0 fusion.34
  137.9 3.0 fusion.7
  141.1 3.2 fusion.114
  144.2 3.2 fusion.112
  147.4 3.2 convolution_subtract_fusion.3
  150.6 3.3 convolution_add_fusion.5
  153.9 3.0 fusion.41
  156.9 3.0 fusion.9
  160.5 1.9 fusion.68
  162.4 3.5 all-to-all-start.1
  166.0 42.3 %all-reduce = (f32[256]{0:T(256)S(1)}, f32[5,64]{1,0:T(8,128)S(1)}, f32[64]{0:T(128)S(1)}, f32[64,64]{1,0:T(8,128)S(1)}, f32[64]{0:T(128)S(1)}, /*index=5*/f32[2,64]{1,0:T(2,128)S(1)}) all-reduce(f32[256]{0:T(256)S(1)} %get-tuple-element.33, f32[5,64]{1,0:T(8,128)S(1)} %fusion.158, ...), channel_id=1, replica_groups=mesh['seq'=8,'batch'=4] {'seq','batch'}, use_global_device_ids=true, to_apply=%region_3.4 | all-reduce | flops 4928 | bytes 39424 | tf_op jit(solution)/shard_map/psum | solution.py:237
  209.4 4.1 %all-to-all-start.3 = ((bf16[32,8,256]{2,0,1:T(8,128)(2,1)}), bf16[32,8,256]{2,0,1:T(8,128)(2,1)S(1)}, u32[]{:S(2)}, u32[]{:S(2)}) async-start(bf16[32,8,256]{2,0,1:T(8,128)(2,1)} %get-tuple-element.53), calls=%async_computation.3 | async-start | bytes 262144 | tf_op jit(solution)/shard_map/all_to_all | solution.py:214
  214.0 0.8 copy-done.19
  215.8 3.9 %all-to-all-done.3 = bf16[32,8,256]{2,0,1:T(8,128)(2,1)S(1)} async-done(((bf16[32,8,256]{2,0,1:T(8,128)(2,1)}), bf16[32,8,256]{2,0,1:T(8,128)(2,1)S(1)}, u32[]{:S(2)}, u32[]{:S(2)}) %all-to-all-start.3) | async-done | bytes 131104 | tf_op jit(solution)/shard_map/all_to_all | solution.py:214
  219.8 0.9 fusion.79
  220.8 0.9 copy-done.12
  221.6 1.1 convolution_bitcast_fusion.3
  223.9 1.0 fusion.11
  224.9 130.6 %all-reduce.4.cloned.1.call-done = (f32[256,768]{0,1:T(8,128)}, f32[256,256]{1,0:T(8,128)}, f32[64,256]{1,0:T(8,128)}) async-done(((f32[256,768]{0,1:T(8,128)}, f32[256,256]{1,0:T(8,128)}, f32[64,256]{1,0:T(8,128)}), (f32[256,768]{0,1:T(8,128)}, f32[256,256]{1,0:T(8,128)}, f32[64,256]{1,0:T(8,128)})) %all-reduce.4.cloned.1.call-update) | async-done | bytes 1114128 | tf_op jit(solution)/shard_map/psum | solution.py:237
  355.5 1.2 broadcast_multiply_fusion
  356.7 1.1 copy.88
  357.9 0.7 broadcast_multiply_fusion.1
  (103 shorter events, 13.0 us)
Async XLA Ops:
  7.2 1.0 copy-start
  7.2 2.2 copy-start.13
  7.2 2.2 copy-start.21
  9.4 1.1 copy-start.7
  10.5 42.2 %all-to-all-start = ((bf16[8,32,256]{2,1,0:T(8,128)(2,1)}), bf16[8,32,256]{2,1,0:T(8,128)(2,1)S(1)}, u32[]{:S(2)}, u32[]{:S(2)}) async-start(bf16[8,32,256]{2,1,0:T(8,128)(2,1)} %bitcast.3), calls=%async_computation | async-start | bytes 262144 | tf_op jit(solution)/shard_map/all_to_all | solution.py:180
  17.7 0.7 copy-start.28
  18.4 0.7 copy-start.34
  19.1 87.6 %copy-start.26 = (f32[32]{0:T(128)}, f32[32]{0:T(128)S(1)}, u32[]{:S(2)}) copy-start(f32[32]{0:T(128)S(1)} %dynamic-slice_negate_fusion) | copy-start | bytes 388
  19.1 0.7 copy-start.24
  19.1 0.7 copy-start.33
  19.8 0.6 copy-start.10
  19.8 0.8 copy-start.17
  20.4 0.7 copy-start.29
  21.1 3.2 copy-start.23
  23.5 0.8 copy-start.3
  46.3 2.9 copy-start.35
  52.7 11.7 %all-to-all-start.2 = ((bf16[8,32,256]{2,1,0:T(8,128)(2,1)}), bf16[8,32,256]{2,1,0:T(8,128)(2,1)}, u32[]{:S(2)}, u32[]{:S(2)}) async-start(bf16[8,32,256]{2,1,0:T(8,128)(2,1)} %bitcast.40), calls=%async_computation.2 | async-start | bytes 262144 | tf_op jit(solution)/shard_map/all_to_all | solution.py:181
  80.3 1.9 copy-start.5
  80.3 1.9 copy-start.6
  106.7 4.1 %copy-start.18 = (f32[64,64]{1,0:T(8,128)S(1)}, f32[64,64]{1,0:T(8,128)}, u32[]{:S(2)}) copy-start(f32[64,64]{1,0:T(8,128)} %param.19) | copy-start | bytes 49156
  113.7 2.9 copy-start.4
  113.7 2.9 copy-start.27
  113.7 5.9 %copy-start.11 = (f32[5,2048]{1,0:T(8,128)S(1)}, f32[5,2048]{1,0:T(8,128)}, u32[]{:S(2)}) copy-start(f32[5,2048]{1,0:T(8,128)} %copy-done.10) | copy-start | bytes 122884
  116.6 5.2 %copy-start.1 = (f32[32,64,64]{2,1,0:T(8,128)S(1)}, f32[32,64,64]{2,1,0:T(8,128)}, u32[]{:S(2)}) copy-start(f32[32,64,64]{2,1,0:T(8,128)} %get-tuple-element.45) | copy-start | bytes 1572868
  121.8 3.2 copy-start.2
  159.9 0.7 copy-start.30
  160.5 5.4 %copy-start.25 = (f32[64]{0:T(128)S(1)}, f32[64]{0:T(128)}, u32[]{:S(2)}) copy-start(f32[64]{0:T(128)} %get-tuple-element.20) | copy-start | bytes 772
  160.5 5.4 %copy-start.32 = (f32[64]{0:T(128)S(1)}, f32[64]{0:T(128)}, u32[]{:S(2)}) copy-start(f32[64]{0:T(128)} %get-tuple-element.46) | copy-start | bytes 772
  160.5 5.4 %copy-start.20 = (f32[64,64]{1,0:T(8,128)S(1)}, f32[64,64]{1,0:T(8,128)}, u32[]{:S(2)}) copy-start(f32[64,64]{1,0:T(8,128)} %fusion.57) | copy-start | bytes 49156
  160.5 5.4 %copy-start.31 = (f32[64]{0:T(128)S(1)}, f32[64]{0:T(128)}, u32[]{:S(2)}) copy-start(f32[64]{0:T(128)} %get-tuple-element.31) | copy-start | bytes 772
  162.4 57.3 %copy-start.8 = (bf16[256,768]{0,1:T(8,128)(2,1)S(1)}, bf16[256,768]{0,1:T(8,128)(2,1)}, u32[]{:S(2)}) copy-start(bf16[256,768]{0,1:T(8,128)(2,1)} %copy-done.7) | copy-start | bytes 1179652
  162.4 47.0 %all-to-all-start.1 = ((bf16[32,8,256]{2,0,1:T(8,128)(2,1)}), bf16[32,8,256]{2,0,1:T(8,128)(2,1)S(1)}, u32[]{:S(2)}, u32[]{:S(2)}) async-start(bf16[32,8,256]{2,0,1:T(8,128)(2,1)} %get-tuple-element.52), calls=%async_computation.1 | async-start | bytes 262144 | tf_op jit(solution)/shard_map/all_to_all | solution.py:213
  209.4 10.3 %all-to-all-start.3 = ((bf16[32,8,256]{2,0,1:T(8,128)(2,1)}), bf16[32,8,256]{2,0,1:T(8,128)(2,1)S(1)}, u32[]{:S(2)}, u32[]{:S(2)}) async-start(bf16[32,8,256]{2,0,1:T(8,128)(2,1)} %get-tuple-element.53), calls=%async_computation.3 | async-start | bytes 262144 | tf_op jit(solution)/shard_map/all_to_all | solution.py:214
  213.5 142.1 %all-reduce.4.cloned.1.call-start = ((), (), s32[]{:S(2)}) async-start(), calls=%async_computation.4 | async-start | bytes 2228224 | tf_op jit(solution)/shard_map/psum | solution.py:237
  214.0 0.8 copy-start.19
  215.2 4.6 %copy-start.15 = (f32[64,256]{1,0:T(8,128)}, f32[64,256]{1,0:T(8,128)S(1)}, u32[]{:S(2)}) copy-start(f32[64,256]{1,0:T(8,128)S(1)} %dynamic_update_slice.3) | copy-start | bytes 196612
  215.8 4.0 %copy-start.14 = (bf16[1,256,256]{2,1,0:T(8,128)(2,1)S(1)}, bf16[1,256,256]{2,1,0:T(8,128)(2,1)}, u32[]{:S(2)}) copy-start(bf16[1,256,256]{2,1,0:T(8,128)(2,1)} %param.13) | copy-start | bytes 393220
  219.8 1.0 copy-start.9
  220.7 0.9 copy-start.12
  356.7 1.2 copy-start.16
  357.9 0.8 copy-start.22
Sparse Core Ops, SparseCore 0:
  222.9 132.5 all-reduce.3
where the time goes:
time: 371 us; the launch traced here: 366 us
  waiting for transfers between devices  139 us (37%)
  matrix products  128 us (35%)
  blocking collectives  42.3 us (11%)
  starting transfers between devices  19.4 us (5%)
  between operations  14.7 us (4%)
  local copies, waits for them, and re-layouts  13.5 us (4%)
  other arithmetic  8.97 us (2%)
    psum x1, waiting for transfers between devices, shards(): lax.psum((grad_in_weight, grad_out_weight, bias_part, filter_grads[0], fi...  131 us
    dot_general x24, matrix products, right_multiply(): return jnp.einsum('...km,mj->...kj', stack_part, table, precision=highest)  77.9 us
    psum x1, blocking collectives, shards(): lax.psum((grad_in_weight, grad_out_weight, bias_part, filter_grads[0], fi...  42.3 us
    dot_general x3, matrix products, inverse(): jnp.einsum('nk,...km->...nm', outer_sin[:half_len], imag_twist, precision...  9.73 us
    dot_general x3, matrix products, inverse(): jnp.einsum('nk,...km->...nm', outer_cos[:half_len], real_twist, precision...  8.86 us
    dot_general x3, matrix products, contract_last(): lax.dot_general(left_side, right_side, (((1,), (1,)), ((), ())), precisio...  8.13 us
    unnamed x73, local copies, waits for them, and re-layouts  7.75 us
  transfers between devices with their start and end apart: 5, of which 3 were waited for; matrix products, arithmetic and copies ran while one was open for 11% of the time, Pallas kernels for 0%

commit v1 on v0

v1 whole, which is shorter than its diff:
```python
import functools
import math

import jax
import jax.numpy as jnp
import numpy as np
from jax import lax
from jax.experimental import pallas as pl
from jax.experimental.pallas import tpu as pltpu
from jax.sharding import PartitionSpec as P

highest = lax.Precision.HIGHEST
MESH = pl.DeviceIdType.MESH
LANES = 128


def factor(length):
    total = 2 * length
    first_len = 2
    while first_len * first_len < total and total % (2 * first_len) == 0:
        first_len = first_len * 2
    return first_len, total // first_len


def make_tables(length):
    total = 2 * length
    first_len, second_len = factor(length)
    half = first_len // 2
    kept = half + 1
    pad = -(-kept // 8) * 8
    k1 = np.arange(kept)[None, :, None]
    n1 = np.arange(half)[None, None, :]
    n2 = np.arange(second_len)[:, None, None]
    angle = 2.0 * np.pi * ((k1 * (n1 * second_len + n2)) % total) / total
    fwd = np.zeros((second_len, 2 * pad, half), np.float32)
    fwd[:, :kept] = np.cos(angle)
    fwd[:, pad : pad + kept] = -np.sin(angle)
    weight = np.where((k1 == 0) | (k1 == half), 1.0, 2.0) / total
    inv = np.zeros((second_len, half, 2 * pad), np.float32)
    inv[:, :, :kept] = np.swapaxes(weight * np.cos(angle), 1, 2)
    inv[:, :, pad : pad + kept] = np.swapaxes(-weight * np.sin(angle), 1, 2)
    index = np.arange(second_len)
    small = 2.0 * np.pi * ((index[:, None] * index[None, :]) % second_len) / second_len
    cos, sin = np.cos(small), np.sin(small)
    inner = np.block([[cos, sin], [-sin, cos]])
    outer = np.block([[cos, -sin], [sin, cos]])
    return tuple(jnp.asarray(t, jnp.bfloat16) for t in (fwd, inv, inner, outer))


def lane_roll(value, shift):
    shift = shift % LANES
    return value if shift == 0 else pltpu.roll(value, shift, 1)


def conv_kernel(
    axis_n,
    chan,
    scale,
    tok,
    og,
    inw,
    outw,
    filt,
    skip,
    fwd,
    inv,
    inner,
    outer,
    gt_out,
    pk_out,
    y_out,
    bias_out,
    send_one,
    recv_one,
    send_two,
    recv_two,
    gates,
    x_buf,
    z_buf,
    v_buf,
    conv_buf,
    sems,
):
    n = axis_n
    me = lax.axis_index("seq")
    pos, width = tok.shape
    rows = send_one.shape[1]
    fold = pos // rows
    step = 2 * chan
    second_len, double_pad, half = fwd.shape
    pad = double_pad // 2
    kept = half + 1
    f32, bf16 = jnp.float32, jnp.bfloat16

    barrier = pltpu.get_barrier_semaphore()
    for k in range(1, n):
        pl.semaphore_signal(
            barrier, inc=1, device_id={"seq": lax.rem(me + k, n)}, device_id_type=MESH
        )

    proj = jnp.dot(tok[...], inw[...], preferred_element_type=f32)
    gate_out = proj[:, :width].astype(bf16)
    gate_in = proj[:, width : 2 * width].astype(bf16)
    values = proj[:, 2 * width :].astype(bf16)
    gated_grad = lax.dot_general(
        og[...], outw[...], (((1,), (1,)), ((), ())), preferred_element_type=f32
    ).astype(bf16)
    gates[0] = gate_out
    gates[1] = gate_in
    gates[2] = values
    gates[3] = gated_grad
    mixed = (values.astype(f32) * gate_in.astype(f32)).astype(bf16).astype(f32)
    grad = (gated_grad.astype(f32) * gate_out.astype(f32)).astype(bf16).astype(f32)
    bias_out[...] = jnp.sum(mixed * grad, axis=0, keepdims=True)

    lane = lax.broadcasted_iota(jnp.int32, (rows, LANES), 1)
    lane_full = lax.broadcasted_iota(jnp.int32, (pos, LANES), 1)
    for d in range(n):
        tile, off = (d * chan) // LANES * LANES, (d * chan) % LANES
        both = jnp.where(
            lane_full < chan,
            lane_roll(mixed[:, tile : tile + LANES], -off),
            lane_roll(grad[:, tile : tile + LANES], chan - off),
        )
        packed = both[:rows]
        for j in range(1, fold):
            packed = jnp.where(
                lane >= j * step, lane_roll(both[j * rows : (j + 1) * rows], j * step), packed
            )
        send_one[d] = packed.astype(bf16)

    pl.semaphore_wait(barrier, n - 1)

    def copy(send, recv, which, k):
        dest = lax.rem(me + k, n)
        return pltpu.make_async_remote_copy(
            src_ref=send.at[dest],
            dst_ref=recv.at[me],
            send_sem=sems.at[2 * which, k],
            recv_sem=sems.at[2 * which + 1, k],
            device_id={"seq": dest},
            device_id_type=MESH,
        )

    for k in range(1, n):
        copy(send_one, recv_one, 0, k).start()
    recv_one[me] = send_one[me]
    v_buf[...] = jnp.zeros_like(v_buf)
    for k in range(1, n):
        copy(send_one, recv_one, 0, k).wait()

    for s in range(n):
        block = recv_one[s].astype(f32)
        for j in range(fold):
            at = pl.ds(s * pos + j * rows, rows)
            x_buf[at, :] = jnp.where(lane < step, lane_roll(block, -j * step), filt[at, :])

    def stage_one(n2, _):
        part = x_buf[pl.ds(n2, half, stride=second_len), :].astype(bf16)
        z_buf[pl.ds(pl.multiple_of(n2 * double_pad, 8), double_pad), :] = jnp.dot(
            fwd[n2], part, preferred_element_type=f32
        )
        return 0

    lax.fori_loop(0, second_len, stage_one, 0, unroll=8)

    lane_k = lax.broadcasted_iota(jnp.int32, (second_len, LANES), 1)
    low = lane_k < step
    mid = (lane_k >= chan) & (lane_k < step)
    sign = jnp.where((lane_k >= chan), -1.0, 1.0).astype(f32)

    def stage_two(k1, _):
        stacked = jnp.concatenate(
            [
                z_buf[pl.ds(k1, second_len, stride=double_pad), :],
                z_buf[pl.ds(pad + k1, second_len, stride=double_pad), :],
            ],
            axis=0,
        ).astype(bf16)
        spec = jnp.dot(inner[...], stacked, preferred_element_type=f32)
        re, im = spec[:second_len], spec[second_len:]
        left_re = jnp.where(low, re, lane_roll(re, chan))
        left_im = jnp.where(low, im, lane_roll(im, chan))
        right_re = jnp.where(mid, lane_roll(re, -chan), lane_roll(re, -step))
        right_im = jnp.where(mid, lane_roll(im, -chan), lane_roll(im, -step)) * sign
        corr_re = jnp.where(lane_k < step, right_re, lane_roll(re, step))
        corr_im = jnp.where(lane_k < step, right_im, lane_roll(im, step) * sign)
        out = jnp.concatenate(
            [
                left_re * corr_re - left_im * corr_im,
                left_re * corr_im + left_im * corr_re,
            ],
            axis=0,
        ).astype(bf16)
        back = jnp.dot(outer[...], out, preferred_element_type=f32)
        v_buf[pl.ds(k1, second_len, stride=double_pad), :] = back[:second_len]
        v_buf[pl.ds(pad + k1, second_len, stride=double_pad), :] = back[second_len:]
        return 0

    unroll = 3 if kept % 3 == 0 else 5 if kept % 5 == 0 else 1
    lax.fori_loop(0, kept, stage_two, 0, unroll=unroll)

    def stage_three(n2, _):
        part = v_buf[pl.ds(pl.multiple_of(n2 * double_pad, 8), double_pad), :].astype(bf16)
        at = pl.ds(n2, half, stride=second_len)
        y_out[at, :] = (
            jnp.dot(inv[n2], part, preferred_element_type=f32) + skip[...] * x_buf[at, :]
        )
        return 0

    lax.fori_loop(0, second_len, stage_three, 0, unroll=8)

    for d in range(n):
        packed = y_out[pl.ds(d * pos, rows), :]
        for j in range(1, fold):
            packed = jnp.where(
                lane >= j * step,
                lane_roll(y_out[pl.ds(d * pos + j * rows, rows), :], j * step),
                packed,
            )
        send_two[d] = packed.astype(bf16)
    for k in range(1, n):
        copy(send_two, recv_two, 1, k).start()
    recv_two[me] = send_two[me]
    for k in range(1, n):
        copy(send_two, recv_two, 1, k).wait()

    per_tile = LANES // chan
    for tile in range(width // LANES):
        for j in range(fold):
            conv_acc = jnp.zeros((rows, LANES), f32)
            grad_acc = jnp.zeros((rows, LANES), f32)
            for i in range(per_tile):
                block = recv_two[tile * per_tile + i].astype(f32)
                own = (lane >= i * chan) & (lane < (i + 1) * chan)
                conv_acc = jnp.where(own, lane_roll(block, i * chan - j * step), conv_acc)
                grad_acc = jnp.where(own, lane_roll(block, i * chan - j * step - chan), grad_acc)
            at = pl.ds(j * rows, rows)
            conv_buf[0, at, tile * LANES : (tile + 1) * LANES] = conv_acc
            conv_buf[1, at, tile * LANES : (tile + 1) * LANES] = grad_acc

    conv = conv_buf[0]
    grad_mixed = conv_buf[1]
    gated = (gates[0].astype(f32) * conv).astype(bf16)
    grad_proj = jnp.concatenate(
        [
            (gates[3].astype(f32) * conv).astype(bf16),
            (grad_mixed * gates[2].astype(f32)).astype(bf16),
            (grad_mixed * gates[1].astype(f32)).astype(bf16),
        ],
        axis=1,
    )
    first = (((0,), (0,)), ((), ()))
    grad_in = lax.dot_general(tok[...], grad_proj, first, preferred_element_type=f32) * scale
    grad_out = lax.dot_general(gated, og[...], first, preferred_element_type=f32) * scale
    at = 0
    for block in (grad_in, grad_out):
        for j in range(block.shape[1] // LANES):
            pk_out[at : at + width, :] = block[:, j * LANES : (j + 1) * LANES].astype(bf16)
            at += width
    gt_out[...] = lax.dot_general(
        grad_proj, inw[...], (((1,), (1,)), ((), ())), preferred_element_type=f32
    ).astype(bf16)


def sum_kernel(ns, nb, a_in, b_in, a_out, b_out, *scratch):
    me_s, me_b = lax.axis_index("seq"), lax.axis_index("batch")
    sems = scratch[-1]
    barrier = pltpu.get_barrier_semaphore()
    for axis, me, n in (("seq", me_s, ns), ("batch", me_b, nb)):
        for k in range(1, n):
            pl.semaphore_signal(
                barrier, inc=1, device_id={axis: lax.rem(me + k, n)}, device_id_type=MESH
            )
    pl.semaphore_wait(barrier, ns + nb - 2)

    def remote(src, dst, phase, k, which, axis, dest):
        return pltpu.make_async_remote_copy(
            src_ref=src,
            dst_ref=dst,
            send_sem=sems.at[phase, 0, k, which],
            recv_sem=sems.at[phase, 1, k, which],
            device_id={axis: dest},
            device_id_type=MESH,
        )

    streams = []
    for which, (src, out) in enumerate(((a_in, a_out), (b_in, b_out))):
        streams.append((which, src, out) + scratch[4 * which : 4 * which + 4])

    def run(make):
        for k, items in make:
            for item in items:
                item.start()
        for k, items in make:
            for item in items:
                item.wait()

    def ds(start, size, unit):
        return pl.ds(pl.multiple_of(start, unit), size)

    def unit_of(ref):
        return 16 if ref.dtype == jnp.bfloat16 else 8

    run(
        [
            (
                k,
                [
                    remote(
                        src.at[ds(lax.rem(me_b + k, nb) * got.shape[1], got.shape[1], unit_of(src))],
                        got.at[k - 1],
                        0,
                        k,
                        which,
                        "batch",
                        lax.rem(me_b + k, nb),
                    )
                    for which, src, out, got, part, got_two, whole in streams
                ],
            )
            for k in range(1, nb)
        ]
    )
    for which, src, out, got, part, got_two, whole in streams:
        size = got.shape[1]
        total = src[ds(me_b * size, size, unit_of(src)), :].astype(jnp.float32)
        for k in range(1, nb):
            total = total + got[k - 1].astype(jnp.float32)
        part[...] = total.astype(part.dtype)
    run(
        [
            (
                k,
                [
                    remote(
                        part.at[
                            ds(lax.rem(me_s + k, ns) * got_two.shape[1], got_two.shape[1], unit_of(src))
                        ],
                        got_two.at[k - 1],
                        1,
                        k,
                        which,
                        "seq",
                        lax.rem(me_s + k, ns),
                    )
                    for which, src, out, got, part, got_two, whole in streams
                ],
            )
            for k in range(1, ns)
        ]
    )
    for which, src, out, got, part, got_two, whole in streams:
        size = got_two.shape[1]
        total = part[ds(me_s * size, size, unit_of(src)), :].astype(jnp.float32)
        for k in range(1, ns):
            total = total + got_two[k - 1].astype(jnp.float32)
        whole[ds(me_b * part.shape[0] + me_s * size, size, unit_of(src)), :] = total.astype(whole.dtype)

    def spread(phase, axis, me, n, size_of):
        made = []
        for k in range(1, n):
            items = []
            for which, src, out, got, part, got_two, whole in streams:
                size = size_of(part, got_two)
                start = me_b * part.shape[0]
                if axis == "seq":
                    start = start + me_s * size
                at = whole.at[ds(start, size, unit_of(src))]
                items.append(remote(at, at, phase, k, which, axis, lax.rem(me + k, n)))
            made.append((k, items))
        run(made)

    spread(2, "seq", me_s, ns, lambda part, got_two: got_two.shape[1])
    spread(3, "batch", me_b, nb, lambda part, got_two: part.shape[0])
    for which, src, out, got, part, got_two, whole in streams:
        out[...] = whole[...]


def vmem(count):
    return [pl.BlockSpec(memory_space=pltpu.VMEM)] * count


def sine_cosine(angle):
    turns = jnp.round(angle * (1.0 / (2.0 * math.pi)))
    reduced = angle - turns * 6.28125
    reduced = reduced - turns * 0.0019350051879882812
    reduced = reduced - turns * 3.0199157663146e-07
    half = reduced * 0.5
    square = half * half
    sin = half * (
        1.0
        + square
        * (-1.0 / 6 + square * (1.0 / 120 + square * (-1.0 / 5040 + square * (1.0 / 362880 - square / 39916800.0))))
    )
    cos = 1.0 + square * (
        -0.5
        + square
        * (1.0 / 24 + square * (-1.0 / 720 + square * (1.0 / 40320 + square * (-1.0 / 3628800 + square / 479001600.0))))
    )
    return 2.0 * sin * cos, 1.0 - 2.0 * sin * sin


def embedding(positions, length, band_count):
    scaled = positions / length
    rows_list = [scaled]
    for band_index in range(1, band_count + 1):
        angle = 2.0 * math.pi * band_index * scaled
        sin, cos = sine_cosine(angle)
        rows_list.append(cos)
        rows_list.append(sin)
    return jnp.stack(rows_list, axis=0)


def contract(left, right, dims, precision=highest):
    return lax.dot_general(left, right, ((dims[:1], dims[1:]), ((), ())), precision=precision)


def shards(
    tokens,
    out_grad,
    in_weight,
    out_weight,
    skip_bias,
    embed_weight,
    embed_bias,
    hidden_weight,
    hidden_bias,
    filter_weight,
    sine_freq,
    decay_rate,
):
    f32, bf16 = jnp.float32, jnp.bfloat16
    tok, og = tokens[0], out_grad[0]
    pos, width = tok.shape
    ns, nb = lax.axis_size("seq"), lax.axis_size("batch")
    length = pos * ns
    me = lax.axis_index("seq")
    chan = width // ns
    step = 2 * chan
    start = me * chan
    hid = hidden_weight.shape[0]
    grad_scale = 1.0 / math.sqrt(nb * length)
    filter_scale = grad_scale / 4.0

    def place(part, at):
        return jnp.pad(part, ((0, 0), (at, LANES - at - chan)))

    weight_part = place(lax.dynamic_slice_in_dim(filter_weight, start, chan, 1), step)
    decay_part = lax.dynamic_slice_in_dim(decay_rate, start, chan, 0)[None]
    skip_part = lax.dynamic_slice_in_dim(skip_bias, start, chan, 0)[None]
    skip_row = place(skip_part, 0) + place(skip_part, chan)
    decay_row = place(decay_part, step)
    lane = jnp.arange(LANES)[None]
    own = (lane >= step) & (lane < step + chan)
    positions = jnp.arange(length, dtype=f32)
    modul = jnp.where(own, 4.0 * jnp.exp(-decay_row * positions[:, None]) / math.sqrt(length), 0.0)

    embed_rows = embedding(positions, length, (embed_weight.shape[0] - 1) // 2)
    pre_one = contract(embed_weight, embed_rows, (0, 0)) + embed_bias[:, None]
    act_one, cos_one = sine_cosine(sine_freq[0][:, None] * pre_one)
    pre_two = contract(hidden_weight, act_one, (0, 0)) + hidden_bias[:, None]
    act_two, cos_two = sine_cosine(sine_freq[1][:, None] * pre_two)
    filt = contract(act_two, weight_part, (0, 0)) * modul

    fwd, inv, inner, outer = make_tables(length)
    second_len, double_pad, half = fwd.shape
    fold = LANES // step
    rows = pos // fold
    main_rows = 4 * width * width // LANES
    pair = (ns, rows, LANES)
    spectral = (second_len * double_pad, LANES)
    grad_tokens, main, y, bias_part = pl.pallas_call(
        functools.partial(conv_kernel, ns, chan, grad_scale),
        out_shape=(
            jax.ShapeDtypeStruct((pos, width), bf16),
            jax.ShapeDtypeStruct((main_rows, LANES), bf16),
            jax.ShapeDtypeStruct((length, LANES), f32),
            jax.ShapeDtypeStruct((1, width), f32),
        ),
        in_specs=vmem(10),
        out_specs=tuple(vmem(4)),
        scratch_shapes=[
            pltpu.VMEM(pair, bf16),
            pltpu.VMEM(pair, bf16),
            pltpu.VMEM(pair, bf16),
            pltpu.VMEM(pair, bf16),
            pltpu.VMEM((4, pos, width), bf16),
            pltpu.VMEM((length, LANES), f32),
            pltpu.VMEM(spectral, f32),
            pltpu.VMEM(spectral, f32),
            pltpu.VMEM((2, pos, width), f32),
            pltpu.SemaphoreType.DMA((4, ns)),
        ],
        compiler_params=pltpu.CompilerParams(collective_id=0, has_side_effects=True),
        name="conv",
    )(tok, og, in_weight, out_weight, filt, skip_row, fwd, inv, inner, outer)

    high = lax.Precision.HIGH
    grad_kernel = jnp.where(own, y, 0.0) * modul
    grad_weight_part = contract(act_two, grad_kernel, (1, 0), high)
    grad_act_two = contract(weight_part, grad_kernel, (1, 1), high)
    grad_pre_two = grad_act_two * sine_freq[1][:, None] * cos_two
    grad_freq_two = jnp.sum(grad_act_two * pre_two * cos_two, axis=1)
    grad_hidden_bias = jnp.sum(grad_pre_two, axis=1)
    grad_hidden_weight = contract(act_one, grad_pre_two, (1, 1), high)
    grad_act_one = contract(hidden_weight, grad_pre_two, (1, 0), high)
    grad_pre_one = grad_act_one * sine_freq[0][:, None] * cos_one
    grad_freq_one = jnp.sum(grad_act_one * pre_one * cos_one, axis=1)
    grad_embed_bias = jnp.sum(grad_pre_one, axis=1)
    grad_embed_weight = contract(embed_rows, grad_pre_one, (1, 1), high)

    smalls = [
        grad_hidden_weight,
        grad_embed_weight,
        grad_embed_bias,
        grad_hidden_bias,
        jnp.stack([grad_freq_one, grad_freq_two], axis=0),
    ]
    flat = jnp.concatenate([s.reshape(-1) for s in smalls]) * filter_scale
    flat = jnp.concatenate([flat, bias_part[0] * grad_scale])
    flat_rows = -(-flat.shape[0] // LANES)
    flat = jnp.pad(flat, (0, flat_rows * LANES - flat.shape[0])).reshape(flat_rows, LANES)
    zero = jnp.zeros((hid, width), f32)
    grad_filter_weight = lax.dynamic_update_slice_in_dim(
        zero, grad_weight_part[:, step : step + chan] * filter_scale, start, 1
    )
    tiles = width // LANES
    blocks = [grad_filter_weight[:, j * LANES : (j + 1) * LANES] for j in range(tiles)]
    extra = jnp.concatenate(blocks + [flat], axis=0)
    unit = ns * nb * 8
    extra_rows = -(-extra.shape[0] // unit) * unit
    extra = jnp.pad(extra, ((0, extra_rows - extra.shape[0]), (0, 0)))
    unit = ns * nb * 16
    all_rows = -(-main_rows // unit) * unit
    if all_rows != main_rows:
        main = jnp.pad(main, ((0, all_rows - main_rows), (0, 0)))

    scratch = []
    for count, kind in ((all_rows, bf16), (extra_rows, f32)):
        scratch += [
            pltpu.VMEM((nb - 1, count // nb, LANES), kind),
            pltpu.VMEM((count // nb, LANES), kind),
            pltpu.VMEM((ns - 1, count // nb // ns, LANES), kind),
            pltpu.VMEM((count, LANES), kind),
        ]
    main, extra = pl.pallas_call(
        functools.partial(sum_kernel, ns, nb),
        out_shape=(
            jax.ShapeDtypeStruct((all_rows, LANES), bf16),
            jax.ShapeDtypeStruct((extra_rows, LANES), f32),
        ),
        in_specs=vmem(2),
        out_specs=tuple(vmem(2)),
        scratch_shapes=scratch + [pltpu.SemaphoreType.DMA((4, 2, max(ns, nb), 2))],
        compiler_params=pltpu.CompilerParams(collective_id=1, has_side_effects=True),
        name="sums",
    )(main, extra)

    def unpack(block, columns):
        parts = block.reshape(columns // LANES, -1, LANES)
        return jnp.concatenate([parts[j] for j in range(columns // LANES)], axis=1)

    main = main.astype(f32)
    grad_in = unpack(main[: 3 * width * tiles], 3 * width)
    grad_out = unpack(main[3 * width * tiles : main_rows], width)
    grad_filter = unpack(extra[: hid * tiles], width)
    flat = extra[hid * tiles : hid * tiles + flat_rows].reshape(-1)
    pieces, at = [], 0
    for s in smalls + [skip_bias]:
        pieces.append(flat[at : at + s.size].reshape(s.shape))
        at += s.size
    return (
        grad_tokens[None],
        grad_in,
        grad_out,
        pieces[5],
        pieces[1],
        pieces[2],
        pieces[0],
        pieces[3],
        grad_filter,
        pieces[4],
    )


def solution(mesh):
    batched = P("batch", "seq", None)
    return jax.shard_map(
        shards,
        mesh=mesh,
        in_specs=(batched, batched) + (P(),) * 10,
        out_specs=(batched,) + (P(),) * 9,
        check_vma=False,
    )
```

time: 371 us -> 93.2 us (0.25); the launches traced: 366 us -> 92.7 us
  waiting for transfers between devices: 139 us -> 0 us
  matrix products: 128 us -> 12.4 us
  Pallas kernels: 0 us -> 65.7 us
  blocking collectives: 42.3 us -> 0 us
  starting transfers between devices: 19.4 us -> 0 us
  between operations: 14.7 us -> 0.88 us
  local copies, waits for them, and re-layouts: 13.5 us -> 8.86 us
  other arithmetic: 8.97 us -> 4.9 us
    psum x1 -> x0, waiting for transfers between devices: 131 us -> none  [shards(): lax.psum((grad_in_weight, grad_out_weight, bias_part, filter_grads[0], fi...]
    dot_general x49 -> x8, matrix products: 128 us -> 12.4 us  [contract(): lax.dot_general(left, right, ((dims[:1], dims[1:]), ((), ())), precision=...]
    pallas_call x0 -> x2, Pallas kernels: none -> 65.7 us  [the longest x1 35.3 us: shards(): pl.pallas_call(functools.partial(sum_kernel, ns, nb), out_shape=(jax.Shap...]
    psum x1 -> x0, blocking collectives: 42.3 us -> none  [shards(): lax.psum((grad_in_weight, grad_out_weight, bias_part, filter_grads[0], fi...]
    all_to_all x4 -> x0, starting transfers between devices: 19.4 us -> none  [the longest x1 6.34 us: shards(): lax.all_to_all(mixed.T, 'seq', split_axis=0, concat_axis=1, tiled=True)]
    all_to_all x4 -> x0, waiting for transfers between devices: 8.54 us -> none  [the longest x1 4.66 us: shards(): lax.all_to_all(grad_conv.T, 'seq', split_axis=0, concat_axis=1, tiled=True)]
    unnamed x73 -> x24, local copies, waits for them, and re-layouts: 7.75 us -> 0.76 us
    slice x0 -> x10, local copies, waits for them, and re-layouts: none -> 5.66 us  [the longest x6 3.16 us: shards(): pieces.append(flat[at:at + s.size].reshape(s.shape))]
  transfers between devices with their start and end apart: 5 -> 0, of which waited for: 3 -> 0; matrix products, arithmetic and copies ran while one was open for 11% -> 0% of each run, Pallas kernels for 0% -> 0%
where the time goes in v1:
time: 93.2 us; the launch traced here: 92.7 us
  Pallas kernels  65.7 us (70%)
  matrix products  12.4 us (13%)
  local copies, waits for them, and re-layouts  8.86 us (10%)
  other arithmetic  4.9 us (5%)
    pallas_call x1, Pallas kernels, shards(): pl.pallas_call(functools.partial(sum_kernel, ns, nb), out_shape=(jax.Shap...  35.3 us
    pallas_call x1, Pallas kernels, shards(): pl.pallas_call(functools.partial(conv_kernel, ns, chan, grad_scale), out_...  30.5 us
    dot_general x8, matrix products, contract(): lax.dot_general(left, right, ((dims[:1], dims[1:]), ((), ())), precision=...  12.4 us
    slice x6, local copies, waits for them, and re-layouts, shards(): pieces.append(flat[at:at + s.size].reshape(s.shape))  3.16 us

profile of v1, /device:TPU:1, one launch (start us, length us, event | category | flops | bytes accessed | tf_op | source)
XLA Modules:
  0.0 92.7 jit_solution(4143543535150130858)
XLA Ops:
  0.6 0.0 copy-start
  0.7 0.2 multiply_multiply_fusion.11
  0.8 0.1 fusion.20
  1.0 0.1 stack.8
  1.1 0.8 slice_bitcast_fusion.1
  1.8 0.0 copy-start.3
  1.8 0.0 copy-start.6
  1.9 0.0 copy-start.7
  1.9 0.0 copy-start.8
  1.9 2.0 %multiply_multiply_fusion.3 = (f32[64,2048]{1,0:T(8,128)S(1)}, f32[2048,64]{0,1:T(8,128)S(1)}) fusion(f32[64]{0:T(128)S(1)} %get-tuple-element.38, f32[64]{0:T(128)} %param.22, f32[5,2048]{1,0:T(8,128)S(1)} %stack.8, f32[5,64]{1,0:T(8,128)} %param.21), kind=kOutput, calls=%fused_computation.11 | convolution fusion | flops 12713984 | bytes 1091328 | tf_op jit(solution)/shard_map/dot_general | solution.py:416
  3.8 0.0 copy-done.3
  3.8 0.0 copy-done.6
  3.8 0.6 fusion
  4.5 0.0 copy-done.7
  4.5 0.0 copy-done.8
  4.5 0.1 dynamic-slice_bitcast_fusion
  4.6 0.1 negate_bitcast_fusion
  4.7 0.0 copy-done
  4.7 0.1 constant_dynamic-slice_fusion
  4.7 3.5 %convolution_multiply_fusion.filt = f32[2048,128]{1,0:T(8,128)} fusion(f32[128]{0:T(128)S(1)} %negate_bitcast_fusion, pred[128]{0:T(512)(128)(4,1)S(1)} %compare_and_fusion, f32[64,32]{1,0:T(8,128)S(1)} %constant_dynamic-slice_fusion, f32[64,2048]{1,0:T(8,128)S(1)} %fusion, f32[64]{0:T(128)S(1)} %get-tuple-element.37), kind=kOutput, calls=%fused_computation | convolution fusion | flops 207093760 | bytes 1581952 | tf_op jit(solution)/shard_map/dot_general | solution.py:416
  8.2 0.6 pad_add_fusion.skip
  8.8 30.5 %conv.1 = (bf16[256,256]{1,0:T(8,128)(2,1)}, bf16[2048,128]{1,0:T(8,128)(2,1)}, f32[2048,128]{1,0:T(8,128)}, f32[1,256]{1,0:T(1,128)}) custom-call(bf16[256,256]{1,0:T(8,128)(2,1)} %bitcast.71, bf16[256,256]{1,0:T(8,128)(2,1)} %bitcast.72, bf16[256,768]{1,0:T(8,128)(2,1)} %inw.1, bf16[256,256]{1,0:T(8,128)(2,1)} %outw.1, ...), custom_call_target="tpu_custom_call" | custom-call | tf_op jit(solution)/shard_map/conv/pallas_call | solution.py:473
  39.3 1.7 %select_multiply_fusion = f32[2048,128]{1,0:T(8,128)S(1)} fusion(f32[2048,128]{1,0:T(8,128)} %get-tuple-element.18, f32[128]{0:T(128)S(1)} %negate_bitcast_fusion, pred[128]{0:T(512)(128)(4,1)S(1)} %compare_and_fusion), kind=kLoop, calls=%fused_computation.6 | loop fusion | flops 1310720 | bytes 2097792 | tf_op jit(solution)/shard_map/mul | solution.py:500
  41.0 1.2 %fusion.31 = (f32[64]{0:T(128)S(1)}, f32[64,2048]{1,0:T(8,128)S(1)}, f32[64]{0:T(128)S(1)}) fusion(f32[64,2048]{1,0:T(8,128)S(1)} %fusion, f32[64]{0:T(128)S(1)} %get-tuple-element.37, f32[2048,128]{1,0:T(8,128)S(1)} %select_multiply_fusion, f32[64,32]{1,0:T(8,128)S(1)} %constant_dynamic-slice_fusion), kind=kOutput, calls=%fused_computation.91 | convolution fusion | flops 104726400 | bytes 2106112 | tf_op jit(solution)/shard_map/dot_general | solution.py:416
  42.2 1.7 %fusion.4 = (f32[64]{0:T(128)S(1)}, f32[64]{0:T(128)S(1)}, f32[2048,64]{0,1:T(8,128)}) fusion(f32[2048,64]{0,1:T(8,128)S(1)} %get-tuple-element.40, f32[64]{0:T(128)S(1)} %get-tuple-element.38, f32[64,2048]{1,0:T(8,128)S(1)} %get-tuple-element.25, f32[64,64]{1,0:T(8,128)S(1)} %copy-done.3), kind=kOutput, calls=%fused_computation.15 | convolution fusion | flops 54394752 | bytes 1590016 | tf_op jit(solution)/shard_map/dot_general | solution.py:416
  43.9 0.1 reshape.335
  44.0 0.0 copy-start.5
  44.0 1.9 %fusion.30 = f32[5,64]{1,0:T(8,128)S(1)} fusion(f32[5,2048]{1,0:T(8,128)S(1)} %stack.8, f32[2048,64]{0,1:T(8,128)} %get-tuple-element.41, f32[64]{0:T(128)S(1)} %get-tuple-element.38, f32[2048,64]{0,1:T(8,128)S(1)} %get-tuple-element.40), kind=kOutput, calls=%fused_computation.90 | convolution fusion | flops 7471104 | bytes 1091072 | tf_op jit(solution)/shard_map/dot_general | solution.py:416
  45.9 0.1 reshape.334
  46.0 0.4 fusion.37
  46.4 0.1 reshape.333
  46.4 0.1 concatenate.18
  46.5 0.0 copy-done.5
  46.5 0.1 fusion.19
  46.6 1.1 %convolution_multiply_fusion.1 = f32[64,32]{1,0:T(8,128)S(1)} fusion(f32[2048,128]{1,0:T(8,128)S(1)} %select_multiply_fusion, f32[64,2048]{1,0:T(8,128)S(1)} %fusion, f32[64]{0:T(128)S(1)} %get-tuple-element.37), kind=kOutput, calls=%fused_computation.4 | convolution fusion | flops 29886464 | bytes 1581312 | tf_op jit(solution)/shard_map/dot_general | solution.py:416
  47.8 0.4 dynamic_update_slice.3
  48.2 0.7 select_maximum_fusion.b_in
  48.9 35.3 %sums.1 = (bf16[2048,128]{1,0:T(8,128)(2,1)}, f32[256,128]{1,0:T(8,128)}) custom-call(bf16[2048,128]{1,0:T(8,128)(2,1)} %get-tuple-element.17.a_in, f32[256,128]{1,0:T(8,128)} %select_maximum_fusion.b_in), custom_call_target="tpu_custom_call" | custom-call | tf_op jit(solution)/shard_map/sums/pallas_call | solution.py:547
  84.2 0.0 copy-start.1
  84.2 0.8 fusion.33
  85.0 0.6 pad_maximum_fusion.1
  85.6 0.9 fusion.32
  86.5 0.7 pad_maximum_fusion
  87.2 0.0 copy-done.1
  87.3 0.0 copy-start.2
  87.3 0.1 convert_element_type.15
  87.4 0.0 copy-start.4
  87.5 0.8 fusion.34
  88.2 0.1 slice.112
  88.3 0.6 slice.133
  88.9 0.6 slice.136
  89.4 0.7 slice.115
  90.2 0.7 reshape.338
  90.9 0.6 fusion.36
  91.4 0.6 slice.132
  92.1 0.0 copy-done.2
  92.1 0.7 copy.36
  92.7 0.0 copy-done.4
  (13 shorter events, 0.1 us)
Async XLA Ops:
  0.6 4.0 %copy-start = (f32[64,256]{1,0:T(8,128)S(1)}, f32[64,256]{1,0:T(8,128)}, u32[]{:S(2)}) copy-start(f32[64,256]{1,0:T(8,128)} %param.25) | copy-start | bytes 196612
  1.8 2.0 %copy-start.3 = (f32[64,64]{1,0:T(8,128)S(1)}, f32[64,64]{1,0:T(8,128)}, u32[]{:S(2)}) copy-start(f32[64,64]{1,0:T(8,128)} %param.23) | copy-start | bytes 49156
  1.8 2.0 %copy-start.6 = (f32[64]{0:T(128)S(1)}, f32[64]{0:T(128)}, u32[]{:S(2)}) copy-start(f32[64]{0:T(128)} %param.24) | copy-start | bytes 772
  1.9 2.6 %copy-start.7 = (f32[256]{0:T(256)S(1)}, f32[256]{0:T(256)}, u32[]{:S(2)}) copy-start(f32[256]{0:T(256)} %param.20) | copy-start | bytes 3076
  1.9 2.6 %copy-start.8 = (f32[256]{0:T(256)S(1)}, f32[256]{0:T(256)}, u32[]{:S(2)}) copy-start(f32[256]{0:T(256)} %param.27) | copy-start | bytes 3076
  44.0 2.5 %copy-start.5 = (f32[1,256]{1,0:T(1,128)S(1)}, f32[1,256]{1,0:T(1,128)}, u32[]{:S(2)}) copy-start(f32[1,256]{1,0:T(1,128)} %get-tuple-element.19) | copy-start | bytes 3076
  84.2 3.1 %copy-start.1 = (bf16[2048,128]{1,0:T(8,128)(2,1)S(1)}, bf16[2048,128]{1,0:T(8,128)(2,1)}, u32[]{:S(2)}) copy-start(bf16[2048,128]{1,0:T(8,128)(2,1)} %get-tuple-element.20) | copy-start | bytes 1572868
  87.3 4.8 %copy-start.2 = (bf16[256,256]{1,0:T(8,128)(2,1)S(1)}, bf16[256,256]{1,0:T(8,128)(2,1)}, u32[]{:S(2)}) copy-start(bf16[256,256]{1,0:T(8,128)(2,1)} %get-tuple-element.16) | copy-start | bytes 393220
  87.4 5.3 %copy-start.4 = (f32[256,768]{1,0:T(8,128)}, f32[256,768]{1,0:T(8,128)S(1)}, u32[]{:S(2)}) copy-start(f32[256,768]{1,0:T(8,128)S(1)} %slice_dynamic-update-slice_fusion) | copy-start | bytes 2359300

commit v2 on v1

v2 whole, which is shorter than its diff:
```python
import functools
import math

import jax
import jax.numpy as jnp
import numpy as np
from jax import lax
from jax.experimental import pallas as pl
from jax.experimental.pallas import tpu as pltpu
from jax.sharding import PartitionSpec as P

highest = lax.Precision.HIGHEST
MESH = pl.DeviceIdType.MESH
LANES = 128
VMEM_BYTES = 66 * 1000 * 1000


def factor(length):
    total = 2 * length
    first_len = 2
    while first_len * first_len < total and total % (2 * first_len) == 0:
        first_len = first_len * 2
    return first_len, total // first_len


def make_tables(length):
    total = 2 * length
    first_len, second_len = factor(length)
    half = first_len // 2
    kept = half + 1
    pad = -(-kept // 8) * 8
    k1 = np.arange(kept)[None, :, None]
    n1 = np.arange(half)[None, None, :]
    n2 = np.arange(second_len)[:, None, None]
    angle = 2.0 * np.pi * ((k1 * (n1 * second_len + n2)) % total) / total
    fwd = np.zeros((second_len, 2 * pad, half), np.float32)
    fwd[:, :kept] = np.cos(angle)
    fwd[:, pad : pad + kept] = -np.sin(angle)
    weight = np.where((k1 == 0) | (k1 == half), 1.0, 2.0) / total
    inv = np.zeros((second_len, half, 2 * pad), np.float32)
    inv[:, :, :kept] = np.swapaxes(weight * np.cos(angle), 1, 2)
    inv[:, :, pad : pad + kept] = np.swapaxes(-weight * np.sin(angle), 1, 2)
    index = np.arange(second_len)
    small = 2.0 * np.pi * ((index[:, None] * index[None, :]) % second_len) / second_len
    cos, sin = np.cos(small), np.sin(small)
    inner = np.block([[cos, sin], [-sin, cos]])
    outer = np.block([[cos, -sin], [sin, cos]])
    return tuple(jnp.asarray(t, jnp.bfloat16) for t in (fwd, inv, inner, outer))


def lane_roll(value, shift):
    shift = shift % LANES
    return value if shift == 0 else pltpu.roll(value, shift, 1)


def dot_as(left, right, dims):
    return lax.dot_general(
        left,
        right,
        ((dims[:1], dims[1:]), ((), ())),
        precision=highest,
        preferred_element_type=jnp.float32,
    )


def step_kernel(
    axis_n,
    batch_n,
    chan,
    scale,
    tok,
    og,
    inw,
    outw,
    embed,
    embed_w,
    columns,
    hidden_w,
    filter_w,
    rates,
    fwd,
    inv,
    inner,
    outer,
    gt_out,
    a_out,
    b_out,
    send_one,
    recv_one,
    send_two,
    recv_two,
    gates,
    x_buf,
    y_out,
    z_buf,
    v_buf,
    net,
    conv_buf,
    sems,
    pk_out,
    extra,
    *sum_scratch,
):
    n = axis_n
    me = lax.axis_index("seq")
    pos, width = tok.shape
    rows = send_one.shape[1]
    fold = pos // rows
    step = 2 * chan
    second_len, double_pad, half = fwd.shape
    pad = double_pad // 2
    kept = half + 1
    f32, bf16 = jnp.float32, jnp.bfloat16

    barrier = pltpu.get_barrier_semaphore()
    for axis, own_at, count in (("seq", me, n), ("batch", lax.axis_index("batch"), batch_n)):
        for k in range(1, count):
            pl.semaphore_signal(
                barrier, inc=1, device_id={axis: lax.rem(own_at + k, count)}, device_id_type=MESH
            )

    proj = jnp.dot(tok[...], inw[...], preferred_element_type=f32)
    gate_out = proj[:, :width].astype(bf16)
    gate_in = proj[:, width : 2 * width].astype(bf16)
    values = proj[:, 2 * width :].astype(bf16)
    gated_grad = lax.dot_general(
        og[...], outw[...], (((1,), (1,)), ((), ())), preferred_element_type=f32
    ).astype(bf16)
    gates[0] = gate_out
    gates[1] = gate_in
    gates[2] = values
    gates[3] = gated_grad
    mixed = (values.astype(f32) * gate_in.astype(f32)).astype(bf16).astype(f32)
    grad = (gated_grad.astype(f32) * gate_out.astype(f32)).astype(bf16).astype(f32)
    bias_sum = jnp.sum(mixed * grad, axis=0, keepdims=True) * scale

    lane = lax.broadcasted_iota(jnp.int32, (rows, LANES), 1)
    lane_full = lax.broadcasted_iota(jnp.int32, (pos, LANES), 1)
    for d in range(n):
        tile, off = (d * chan) // LANES * LANES, (d * chan) % LANES
        both = jnp.where(
            lane_full < chan,
            lane_roll(mixed[:, tile : tile + LANES], -off),
            lane_roll(grad[:, tile : tile + LANES], chan - off),
        )
        packed = both[:rows]
        for j in range(1, fold):
            packed = jnp.where(
                lane >= j * step, lane_roll(both[j * rows : (j + 1) * rows], j * step), packed
            )
        send_one[d] = packed.astype(bf16)

    pl.semaphore_wait(barrier, n + batch_n - 2)

    def copy(send, recv, which, k):
        dest = lax.rem(me + k, n)
        return pltpu.make_async_remote_copy(
            src_ref=send.at[dest],
            dst_ref=recv.at[me],
            send_sem=sems.at[2 * which, k],
            recv_sem=sems.at[2 * which + 1, k],
            device_id={"seq": dest},
            device_id_type=MESH,
        )

    for k in range(1, n):
        copy(send_one, recv_one, 0, k).start()
    recv_one[me] = send_one[me]
    v_buf[...] = jnp.zeros_like(v_buf)
    extra[...] = jnp.zeros_like(extra)
    length = x_buf.shape[0]
    hid = hidden_w.shape[0]
    tiles = width // LANES

    def select_own(value, target):
        lane_v = lax.broadcasted_iota(jnp.int32, (value.shape[0], LANES), 1)
        got = jnp.zeros((value.shape[0], LANES), f32)
        for i in range(n):
            tile, off = (i * chan) // LANES * LANES, (i * chan) % LANES
            part = lane_roll(value[:, tile : tile + LANES], target - off)
            got = jnp.where(jnp.logical_and(me == i, lane_v >= 0), part, got)
        return jnp.where((lane_v >= target) & (lane_v < target + chan), got, 0.0)

    weight = select_own(filter_w[...], step)
    rate = select_own(rates[...], step)
    skip_at = select_own(rates[...], 0) + select_own(rates[...], chan)
    decay, skip = rate[0:1], skip_at[1:2]
    freq_one, freq_two = columns[:, 0:1], columns[:, 1:2]
    tile_rows = min(256, length)

    def modulation(at_row):
        time = (lax.broadcasted_iota(jnp.int32, (tile_rows, LANES), 0) + at_row).astype(f32)
        return jnp.exp(-decay * time) * (4.0 / math.sqrt(length))

    def net_forward(i, _):
        at = pl.ds(pl.multiple_of(i * tile_rows, tile_rows), tile_rows)
        pre_one = dot_as(embed_w[...], embed[:, at], (0, 0)) + columns[:, 2:3]
        act_one, cos_one = sine_cosine(freq_one * pre_one)
        pre_two = dot_as(hidden_w[...], act_one, (0, 0)) + columns[:, 3:4]
        act_two, cos_two = sine_cosine(freq_two * pre_two)
        net[0, :, at] = pre_one
        net[1, :, at] = act_one
        net[2, :, at] = cos_one
        net[3, :, at] = pre_two
        net[4, :, at] = act_two
        net[5, :, at] = cos_two
        y_out[at, :] = dot_as(act_two, weight, (0, 0)) * modulation(i * tile_rows)
        return 0

    lax.fori_loop(0, length // tile_rows, net_forward, 0)
    for k in range(1, n):
        copy(send_one, recv_one, 0, k).wait()

    for s in range(n):
        block = recv_one[s].astype(f32)
        for j in range(fold):
            at = pl.ds(s * pos + j * rows, rows)
            x_buf[at, :] = jnp.where(lane < step, lane_roll(block, -j * step), y_out[at, :])

    def stage_one(n2, _):
        part = x_buf[pl.ds(n2, half, stride=second_len), :].astype(bf16)
        z_buf[pl.ds(pl.multiple_of(n2 * double_pad, 8), double_pad), :] = jnp.dot(
            fwd[n2], part, preferred_element_type=f32
        )
        return 0

    lax.fori_loop(0, second_len, stage_one, 0, unroll=8)

    lane_k = lax.broadcasted_iota(jnp.int32, (second_len, LANES), 1)
    low = lane_k < step
    mid = (lane_k >= chan) & (lane_k < step)
    sign = jnp.where((lane_k >= chan), -1.0, 1.0).astype(f32)

    def stage_two(k1, _):
        stacked = jnp.concatenate(
            [
                z_buf[pl.ds(k1, second_len, stride=double_pad), :],
                z_buf[pl.ds(pad + k1, second_len, stride=double_pad), :],
            ],
            axis=0,
        ).astype(bf16)
        spec = jnp.dot(inner[...], stacked, preferred_element_type=f32)
        re, im = spec[:second_len], spec[second_len:]
        left_re = jnp.where(low, re, lane_roll(re, chan))
        left_im = jnp.where(low, im, lane_roll(im, chan))
        right_re = jnp.where(mid, lane_roll(re, -chan), lane_roll(re, -step))
        right_im = jnp.where(mid, lane_roll(im, -chan), lane_roll(im, -step)) * sign
        corr_re = jnp.where(lane_k < step, right_re, lane_roll(re, step))
        corr_im = jnp.where(lane_k < step, right_im, lane_roll(im, step) * sign)
        out = jnp.concatenate(
            [
                left_re * corr_re - left_im * corr_im,
                left_re * corr_im + left_im * corr_re,
            ],
            axis=0,
        ).astype(bf16)
        back = jnp.dot(outer[...], out, preferred_element_type=f32)
        v_buf[pl.ds(k1, second_len, stride=double_pad), :] = back[:second_len]
        v_buf[pl.ds(pad + k1, second_len, stride=double_pad), :] = back[second_len:]
        return 0

    unroll = 3 if kept % 3 == 0 else 5 if kept % 5 == 0 else 1
    lax.fori_loop(0, kept, stage_two, 0, unroll=unroll)

    def stage_three(n2, _):
        part = v_buf[pl.ds(pl.multiple_of(n2 * double_pad, 8), double_pad), :].astype(bf16)
        at = pl.ds(n2, half, stride=second_len)
        y_out[at, :] = (
            jnp.dot(inv[n2], part, preferred_element_type=f32) + skip * x_buf[at, :]
        )
        return 0

    lax.fori_loop(0, second_len, stage_three, 0, unroll=8)

    for d in range(n):
        packed = y_out[pl.ds(d * pos, rows), :]
        for j in range(1, fold):
            packed = jnp.where(
                lane >= j * step,
                lane_roll(y_out[pl.ds(d * pos + j * rows, rows), :], j * step),
                packed,
            )
        send_two[d] = packed.astype(bf16)
    for k in range(1, n):
        copy(send_two, recv_two, 1, k).start()
    recv_two[me] = send_two[me]

    lane_t = lax.broadcasted_iota(jnp.int32, (tile_rows, LANES), 1)
    owned = (lane_t >= step) & (lane_t < step + chan)

    def net_backward(i, carry):
        at = pl.ds(pl.multiple_of(i * tile_rows, tile_rows), tile_rows)
        grad_kernel = jnp.where(owned, y_out[at, :], 0.0) * modulation(i * tile_rows)
        grad_weight = dot_as(net[4, :, at], grad_kernel, (1, 0))
        grad_act_two = dot_as(weight, grad_kernel, (1, 1)) * net[5, :, at]
        grad_pre_two = grad_act_two * freq_two
        grad_hidden = dot_as(net[1, :, at], grad_pre_two, (1, 1))
        grad_act_one = dot_as(hidden_w[...], grad_pre_two, (1, 0)) * net[2, :, at]
        grad_pre_one = grad_act_one * freq_one
        rows_at = embed[:, at]
        new = (
            grad_weight,
            grad_hidden,
            dot_as(rows_at, grad_pre_one, (1, 1)),
            dot_as(rows_at, grad_pre_two, (1, 1)),
            dot_as(rows_at, grad_act_one * net[0, :, at], (1, 1)),
            dot_as(rows_at, grad_act_two * net[3, :, at], (1, 1)),
        )
        return tuple(old + term for old, term in zip(carry, new))

    zeros = lambda r, c: jnp.zeros((r, c), f32)
    em = embed.shape[0]
    sums = lax.fori_loop(
        0,
        length // tile_rows,
        net_backward,
        (zeros(hid, LANES), zeros(hid, hid)) + (zeros(em, hid),) * 4,
    )
    sums = tuple(term * (scale * 0.25) for term in sums)
    lane_h = lax.broadcasted_iota(jnp.int32, (hid, LANES), 1)
    for tile in range(tiles):
        placed = zeros(hid, LANES)
        for i in range(n):
            if (i * chan) // LANES == tile:
                off = (i * chan) % LANES
                mask = (lane_h >= off) & (lane_h < off + chan) & (me == i)
                placed = jnp.where(mask, lane_roll(sums[0], off - step), placed)
        extra[tile * hid : (tile + 1) * hid, :] = placed
    base = tiles * hid
    extra[base : base + hid, 0:hid] = sums[1]
    base += hid
    for term in sums[2:]:
        extra[base : base + em, 0:hid] = term
        base += em
    for tile in range(tiles):
        extra[base + tile : base + tile + 1, :] = bias_sum[:, tile * LANES : (tile + 1) * LANES]

    main_sum = make_sum(n, batch_n, pk_out, a_out, sum_scratch[:5], 0)
    extra_sum = make_sum(n, batch_n, extra, b_out, sum_scratch[5:], 1)
    extra_sum.start(0)
    for k in range(1, n):
        copy(send_two, recv_two, 1, k).wait()

    per_tile = LANES // chan
    for tile in range(width // LANES):
        for j in range(fold):
            conv_acc = jnp.zeros((rows, LANES), f32)
            grad_acc = jnp.zeros((rows, LANES), f32)
            for i in range(per_tile):
                block = recv_two[tile * per_tile + i].astype(f32)
                own = (lane >= i * chan) & (lane < (i + 1) * chan)
                conv_acc = jnp.where(own, lane_roll(block, i * chan - j * step), conv_acc)
                grad_acc = jnp.where(own, lane_roll(block, i * chan - j * step - chan), grad_acc)
            at = pl.ds(j * rows, rows)
            conv_buf[0, at, tile * LANES : (tile + 1) * LANES] = conv_acc
            conv_buf[1, at, tile * LANES : (tile + 1) * LANES] = grad_acc

    conv = conv_buf[0]
    grad_mixed = conv_buf[1]
    gated = (gates[0].astype(f32) * conv).astype(bf16)
    grad_proj = jnp.concatenate(
        [
            (gates[3].astype(f32) * conv).astype(bf16),
            (grad_mixed * gates[2].astype(f32)).astype(bf16),
            (grad_mixed * gates[1].astype(f32)).astype(bf16),
        ],
        axis=1,
    )
    first = (((0,), (0,)), ((), ()))
    grad_in = lax.dot_general(tok[...], grad_proj, first, preferred_element_type=f32) * scale
    grad_out = lax.dot_general(gated, og[...], first, preferred_element_type=f32) * scale
    at = 0
    for block in (grad_in, grad_out):
        for j in range(block.shape[1] // LANES):
            pk_out[at : at + width, :] = block[:, j * LANES : (j + 1) * LANES].astype(bf16)
            at += width
    main_sum.start(0)
    gt_out[...] = lax.dot_general(
        grad_proj, inw[...], (((1,), (1,)), ((), ())), preferred_element_type=f32
    ).astype(bf16)
    for phase in range(4):
        for stream in (extra_sum, main_sum):
            stream.finish(phase)
            if phase < 3:
                stream.start(phase + 1)
            else:
                stream.out[...] = stream.whole[...]


class make_sum:
    def __init__(self, ns, nb, src, out, scratch, which):
        self.ns, self.nb, self.src, self.out, self.which = ns, nb, src, out, which
        self.got, self.part, self.got_two, self.whole, self.sems = scratch
        self.me_s, self.me_b = lax.axis_index("seq"), lax.axis_index("batch")
        self.unit = 16 if src.dtype == jnp.bfloat16 else 8
        self.long, self.short = self.got.shape[1], self.got_two.shape[1]

    def rows(self, start, size):
        return pl.ds(pl.multiple_of(start, self.unit), size)

    def copies(self, phase):
        axis, me, n = (
            ("seq", self.me_s, self.ns) if phase in (1, 2) else ("batch", self.me_b, self.nb)
        )
        made = []
        for k in range(1, n):
            dest = lax.rem(me + k, n)
            if phase == 0:
                src, dst = self.src.at[self.rows(dest * self.long, self.long)], self.got.at[k - 1]
            elif phase == 1:
                src = self.part.at[self.rows(dest * self.short, self.short)]
                dst = self.got_two.at[k - 1]
            else:
                start, size = self.me_b * self.long, self.long
                if phase == 2:
                    start, size = start + self.me_s * self.short, self.short
                src = dst = self.whole.at[self.rows(start, size)]
            made.append(
                pltpu.make_async_remote_copy(
                    src_ref=src,
                    dst_ref=dst,
                    send_sem=self.sems.at[phase, 0, k],
                    recv_sem=self.sems.at[phase, 1, k],
                    device_id={axis: dest},
                    device_id_type=MESH,
                )
            )
        return made

    def start(self, phase):
        for item in self.copies(phase):
            item.start()

    def finish(self, phase):
        for item in self.copies(phase):
            item.wait()
        if phase == 0:
            total = self.src[self.rows(self.me_b * self.long, self.long), :].astype(jnp.float32)
            for k in range(1, self.nb):
                total = total + self.got[k - 1].astype(jnp.float32)
            self.part[...] = total.astype(self.part.dtype)
        if phase == 1:
            total = self.part[self.rows(self.me_s * self.short, self.short), :].astype(jnp.float32)
            for k in range(1, self.ns):
                total = total + self.got_two[k - 1].astype(jnp.float32)
            start = self.me_b * self.long + self.me_s * self.short
            self.whole[self.rows(start, self.short), :] = total.astype(self.whole.dtype)


def unpack_kernel(main, extra, g_in, g_out, skip, emb, emb_b, hidden, hidden_b, filt, freq):
    width = g_out.shape[0]
    hid = hidden.shape[0]
    at = 0
    for ref in (g_in, g_out):
        for j in range(ref.shape[1] // LANES):
            ref[:, j * LANES : (j + 1) * LANES] = main[at : at + width, :].astype(jnp.float32)
            at += width
    tiles = width // LANES
    for j in range(tiles):
        filt[:, j * LANES : (j + 1) * LANES] = extra[j * hid : (j + 1) * hid, :]
    base = tiles * hid
    hidden[...] = extra[base : base + hid, 0:hid]
    base += hid
    count = emb.shape[0]
    em = -(-(count + 1) // 8) * 8
    emb[...] = extra[base : base + count, 0:hid]
    emb_b[...] = extra[base + count : base + count + 1, 0:hid]
    hidden_b[...] = extra[base + em + count : base + em + count + 1, 0:hid]
    freq[0:1, :] = extra[base + 2 * em + count : base + 2 * em + count + 1, 0:hid]
    freq[1:2, :] = extra[base + 3 * em + count : base + 3 * em + count + 1, 0:hid]
    base += 4 * em
    for j in range(tiles):
        skip[:, j * LANES : (j + 1) * LANES] = extra[base + j : base + j + 1, :]


def vmem(count):
    return [pl.BlockSpec(memory_space=pltpu.VMEM)] * count


def sine_cosine(angle):
    turns = jnp.round(angle * (1.0 / (2.0 * math.pi)))
    reduced = angle - turns * 6.28125
    reduced = reduced - turns * 0.0019350051879882812
    reduced = reduced - turns * 3.0199157663146e-07
    half = reduced * 0.5
    square = half * half
    sin = half * (
        1.0
        + square
        * (-1.0 / 6 + square * (1.0 / 120 + square * (-1.0 / 5040 + square * (1.0 / 362880 - square / 39916800.0))))
    )
    cos = 1.0 + square * (
        -0.5
        + square
        * (1.0 / 24 + square * (-1.0 / 720 + square * (1.0 / 40320 + square * (-1.0 / 3628800 + square / 479001600.0))))
    )
    return 2.0 * sin * cos, 1.0 - 2.0 * sin * sin


def embedding(length, count):
    rows = np.zeros((-(-(count + 1) // 8) * 8, length), np.float32)
    scaled = np.arange(length) / length
    rows[0] = scaled
    for band_index in range(1, (count - 1) // 2 + 1):
        rows[2 * band_index - 1] = np.cos(2.0 * np.pi * band_index * scaled)
        rows[2 * band_index] = np.sin(2.0 * np.pi * band_index * scaled)
    rows[count] = 1.0
    return jnp.asarray(rows)


def shards(
    tokens,
    out_grad,
    in_weight,
    out_weight,
    skip_bias,
    embed_weight,
    embed_bias,
    hidden_weight,
    hidden_bias,
    filter_weight,
    sine_freq,
    decay_rate,
):
    f32, bf16 = jnp.float32, jnp.bfloat16
    tok, og = tokens[0], out_grad[0]
    pos, width = tok.shape
    ns, nb = lax.axis_size("seq"), lax.axis_size("batch")
    length = pos * ns
    chan = width // ns
    hid = hidden_weight.shape[0]
    count = embed_weight.shape[0]
    embed = embedding(length, count)
    em = embed.shape[0]
    embed_w = jnp.pad(embed_weight, ((0, em - count), (0, 0)))
    columns = jnp.stack([sine_freq[0], sine_freq[1], embed_bias, hidden_bias], axis=1)
    rates = jnp.stack([decay_rate, skip_bias], axis=0)

    fwd, inv, inner, outer = make_tables(length)
    second_len, double_pad, half = fwd.shape
    rows = pos // (LANES // (2 * chan))
    tiles = width // LANES
    unit = ns * nb * 16
    main_rows = -(-4 * width * tiles // unit) * unit
    unit = ns * nb * 8
    extra_rows = -(-(tiles * hid + hid + 4 * em + tiles) // unit) * unit
    pair = (ns, rows, LANES)
    spectral = (second_len * double_pad, LANES)
    scratch = []
    for total, kind in ((main_rows, bf16), (extra_rows, f32)):
        scratch += [
            pltpu.VMEM((nb - 1, total // nb, LANES), kind),
            pltpu.VMEM((total // nb, LANES), kind),
            pltpu.VMEM((ns - 1, total // nb // ns, LANES), kind),
            pltpu.VMEM((total, LANES), kind),
            pltpu.SemaphoreType.DMA((4, 2, max(ns, nb))),
        ]
    grad_tokens, main, extra = pl.pallas_call(
        functools.partial(step_kernel, ns, nb, chan, 1.0 / math.sqrt(nb * length)),
        out_shape=(
            jax.ShapeDtypeStruct((pos, width), bf16),
            jax.ShapeDtypeStruct((main_rows, LANES), bf16),
            jax.ShapeDtypeStruct((extra_rows, LANES), f32),
        ),
        in_specs=vmem(14),
        out_specs=tuple(vmem(3)),
        scratch_shapes=[
            pltpu.VMEM(pair, bf16),
            pltpu.VMEM(pair, bf16),
            pltpu.VMEM(pair, bf16),
            pltpu.VMEM(pair, bf16),
            pltpu.VMEM((4, pos, width), bf16),
            pltpu.VMEM((length, LANES), f32),
            pltpu.VMEM((length, LANES), f32),
            pltpu.VMEM(spectral, f32),
            pltpu.VMEM(spectral, f32),
            pltpu.VMEM((6, hid, length), f32),
            pltpu.VMEM((2, pos, width), f32),
            pltpu.SemaphoreType.DMA((4, ns)),
            pltpu.VMEM((main_rows, LANES), bf16),
            pltpu.VMEM((extra_rows, LANES), f32),
        ]
        + scratch,
        compiler_params=pltpu.CompilerParams(
            collective_id=0, has_side_effects=True, vmem_limit_bytes=VMEM_BYTES
        ),
        name="step",
    )(
        tok,
        og,
        in_weight,
        out_weight,
        embed,
        embed_w,
        columns,
        hidden_weight,
        filter_weight,
        rates,
        fwd,
        inv,
        inner,
        outer,
    )

    shapes = (
        (width, 3 * width),
        (width, width),
        (1, width),
        (count, hid),
        (1, hid),
        (hid, hid),
        (1, hid),
        (hid, width),
        (2, hid),
    )
    out = pl.pallas_call(
        unpack_kernel,
        out_shape=tuple(jax.ShapeDtypeStruct(shape, f32) for shape in shapes),
        in_specs=vmem(2),
        out_specs=tuple(vmem(len(shapes))),
        name="unpack",
    )(main, extra)
    return (
        grad_tokens[None],
        out[0],
        out[1],
        out[2][0],
        out[3],
        out[4][0],
        out[5],
        out[6][0],
        out[7],
        out[8],
    )


def solution(mesh):
    batched = P("batch", "seq", None)
    return jax.shard_map(
        shards,
        mesh=mesh,
        in_specs=(batched, batched) + (P(),) * 10,
        out_specs=(batched,) + (P(),) * 9,
        check_vma=False,
    )
```

time: 93.2 us -> 70.2 us (0.75)
  matrix products: 12.4 us -> 0 us
  local copies, waits for them, and re-layouts: 8.86 us -> 4.32 us
  other arithmetic: 4.9 us -> 1.96 us
  Pallas kernels: 65.7 us -> 63 us
    dot_general x8 -> x0, matrix products: 12.4 us -> none  [contract(): lax.dot_general(left, right, ((dims[:1], dims[1:]), ((), ())), precision=...]
    slice x10 -> x0, local copies, waits for them, and re-layouts: 5.66 us -> none  [the longest x6 3.16 us: shards(): pieces.append(flat[at:at + s.size].reshape(s.shape))]
    pallas_call x2, Pallas kernels: 65.7 us -> 63 us  [the longest x1 60.9 us: shards(): pl.pallas_call(functools.partial(step_kernel, ns, nb, chan, 1.0 / math.sq...]
    concatenate x3 -> x0, other arithmetic: 2.02 us -> none  [the longest x2 1.35 us: unpack(): return jnp.concatenate([parts[j] for j in range(columns // LANES)], axis=1)]
    mul x5 -> x0, other arithmetic: 1.98 us -> none  [the longest x1 1.71 us: shards(): grad_kernel = jnp.where(own, y, 0.0) * modul]
    another operation x1 -> x2, other arithmetic: 0.01 us -> 1.96 us  [the longest x1 1.28 us: shards(): rates = jnp.stack([decay_rate, skip_bias], axis=0)]
    another operation x1 -> x2, local copies, waits for them, and re-layouts: 0.07 us -> 1.47 us  [shards(): jnp.stack([sine_freq[0], sine_freq[1], embed_bias, hidden_bias], axis=1)]
    pad x0 -> x1, local copies, waits for them, and re-layouts: none -> 1.28 us  [shards(): embed_w = jnp.pad(embed_weight, ((0, em - count), (0, 0)))]
where the time goes in v2:
time: 70.2 us; the launch traced here: 70 us
  Pallas kernels  63 us (90%)
  local copies, waits for them, and re-layouts  4.32 us (6%)
  other arithmetic  1.96 us (3%)
    pallas_call x1, Pallas kernels, shards(): pl.pallas_call(functools.partial(step_kernel, ns, nb, chan, 1.0 / math.sq...  60.9 us
    pallas_call x1, Pallas kernels, shards(): pl.pallas_call(unpack_kernel, out_shape=tuple((jax.ShapeDtypeStruct(shape...  2.11 us
    unnamed x1, local copies, waits for them, and re-layouts  1.57 us
    another operation x2, local copies, waits for them, and re-layouts, shards(): jnp.stack([sine_freq[0], sine_freq[1], embed_bias, hidden_bias], axis=1)  1.47 us

profile of v2, /device:TPU:1, one launch (start us, length us, event | category | flops | bytes accessed | tf_op | source)
XLA Modules:
  0.0 70.0 jit_solution(7816918775638044892)
XLA Ops:
  0.6 0.8 %slice_bitcast_fusion.1 = (f32[64,1]{0,1:T(1,128)S(1)}, f32[64,1]{0,1:T(1,128)S(1)}) fusion(f32[2,64]{1,0:T(2,128)} %param.27), kind=kLoop, calls=%fused_computation.3 | loop fusion | bytes 1024 | tf_op jit(solution)/shard_map/stack;squeeze | solution.py:536
  1.4 0.7 pad_maximum_fusion
  2.1 1.3 %pad_maximum_fusion.1.rates = f32[2,256]{1,0:T(2,128)} fusion(f32[1,256]{1,0:T(1,128)} %bitcast.17, f32[1,256]{1,0:T(1,128)} %bitcast.18), kind=kLoop, calls=%fused_computation.1 | loop fusion | flops 512 | bytes 4096 | tf_op jit(solution)/shard_map/stack | solution.py:537
  3.4 1.3 %pad.4.embed_w = f32[8,64]{1,0:T(8,128)} pad(f32[5,64]{1,0:T(8,128)} %param.22, f32[]{:T(128)} %constant.12.clone.1), padding=0_3x0_0 | pad | bytes 3332 | tf_op jit(solution)/shard_map/jit(_pad)/pad | solution.py:535
  4.6 0.7 %copy.31.columns = f32[64,4]{1,0:T(8,128)} copy(f32[64,4]{0,1:T(4,128)S(1)} %pad_maximum_fusion) | data formatting | bytes 2048 | tf_op jit(solution)/shard_map/stack | solution.py:536
  5.4 60.9 %step.1 = (bf16[256,256]{1,0:T(8,128)(2,1)}, bf16[2048,128]{1,0:T(8,128)(2,1)}, f32[256,128]{1,0:T(8,128)}) custom-call(bf16[256,256]{1,0:T(8,128)(2,1)} %bitcast.14, bf16[256,256]{1,0:T(8,128)(2,1)} %bitcast.15, bf16[256,768]{1,0:T(8,128)(2,1)} %inw.1, bf16[256,256]{1,0:T(8,128)(2,1)} %outw.1, f32[8,2048]{1,0:T(8,128)} %constant.13.clone.embed, ...), custom_call_target="tpu_custom_call" | custom-call | tf_op jit(solution)/shard_map/step/pallas_call | solution.py:558
  66.3 2.1 %unpack.1 = (f32[256,768]{1,0:T(8,128)}, f32[256,256]{1,0:T(8,128)}, f32[1,256]{1,0:T(1,128)}, f32[5,64]{1,0:T(8,128)}, f32[1,64]{1,0:T(1,128)}, /*index=5*/f32[...) custom-call(bf16[2048,128]{1,0:T(8,128)(2,1)} %get-tuple-element.23.main, ...), custom_call_target="tpu_custom_call" | custom-call | tf_op jit(solution)/shard_map/unpack/pallas_call | solution.py:616
  68.4 1.6 %copy.33 = bf16[1,256,256]{2,1,0:T(8,128)(2,1)} copy(bf16[1,256,256]{2,1,0:T(8,128)(2,1)} %bitcast.16) | data formatting | bytes 262144
